TPU v7x, 512 devices: a 4x2x32 block of a 4x8x32 slice. The times are simulated.
512 devices in a mesh: graphs: 2 (over y), rows: 32 (over z), cols: 4 (over x), sub: 2 (over core).
Axes of the slice: x: 4, y: 2, z: 32, core: 2. Of those that a mesh axis runs over, the one named last changes fastest.
The devices are a block of a 4x8x32 slice.
Arguments:
- current_block: float32 [16, 1048576], P(None, ('graphs', 'rows', 'cols', 'sub')), parts along dimension 1, may hold values from -1200 to 1200, as said below
- previous_block: float32 [16, 1048576], P(None, ('graphs', 'rows', 'cols', 'sub')), parts along dimension 1, may hold values from -1200 to 1200, as said below
- adjacency_tiles: float32 [24576, 128, 128], P(('graphs', 'rows', 'cols', 'sub')), parts along dimension 0, may hold values from -0.3125 to 0.3125
- tile_rows: int32 [24576], P(('graphs', 'rows', 'cols', 'sub')), parts along dimension 0, may hold values from 0 to 4095, as said below
- tile_cols: int32 [24576], P(('graphs', 'rows', 'cols', 'sub')), parts along dimension 0, may hold values from 0 to 4095, as said below
- tile_count: int32 [512], P(('graphs', 'rows', 'cols', 'sub')), parts along dimension 0, may hold values from 18 to 48, as said below
- locked: int32 [2], P('graphs'), parts along dimension 0, may hold values from 0 to 7
Outputs:
- w_basis: float32 [16, 1048576], P(None, ('graphs', 'rows', 'cols', 'sub')), parts along dimension 1
- w_image: float32 [16, 1048576], P(None, ('graphs', 'rows', 'cols', 'sub')), parts along dimension 1
- ritz_matrix: float32 [96, 48], P('graphs'), parts along dimension 0
There are 2 independent parts, one for each index of `graphs`. A program takes and returns all parts, laid end to end along the dimension named above; each array names one. Nothing has to cross between parts.
Inputs may be any that keep to these rules, and one draw needn't show every extreme that they name: `current_block`: entries of order one to some hundreds. `previous_block`: entries of order one to some hundreds. Slots d * 48 to (d + 1) * 48 - 1 belong to device d and name its own tile rows d * 16 to (d + 1) * 16 - 1. The first 16 slots of a device name its tile rows in order, with tile_cols equal to tile_rows. Slots past the device's count name tile row d * 16 and carry no weight. `tile_cols`: A slot of device d names a tile column from d * 16 - 8 to (d + 1) * 16 + 7. Slot 16 of a device names a tile of the block before it and slot 17 one of the block after it, where such a block exists. A pair of tile row and tile column may stand in several slots; their tiles add. `tile_count`: in every draw some device has all 48 slots live.
All inputs are finite; a program needn't handle non-finite values.
Results may differ from a plain program's by a relative error of at most 0.000094.
Values sent between devices are 32-bit elements; how exact they have to be, the bound alone decides.
A program may use at most 64 MiB of HBM per device.

v0:
```python
import jax
import jax.numpy as jnp
from jax import lax
from jax.sharding import PartitionSpec as P


def extended(value, sides, width):
    edges = {}
    for axis, dim in sides:
        devices, length = (lax.axis_size(axis), value.shape[dim])
        up = [(i, (i + 1) % devices) for i in range(devices - 1)]
        last = lax.slice_in_dim(value, length - width, length, axis=dim)
        initial = lax.slice_in_dim(value, 0, width, axis=dim)
        edges[dim] = (
            lax.ppermute(last, axis, up),
            lax.ppermute(initial, axis, [(b, a) for a, b in up]),
        )
    done = []
    for _, dim in sides:
        low, high = edges[dim]
        around = [(width, width) if d in done else (0, 0) for d in range(value.ndim)]
        value = jnp.concatenate([jnp.pad(low, around), value, jnp.pad(high, around)], axis=dim)
        done.append(dim)
    return value


def one_axis_at_a_time(value, axes):
    for axis in axes:
        value = lax.psum(value, axis)
    return value


def inner_products(left, right):
    return jnp.dot(left, right.T, precision=lax.Precision.HIGHEST)


def solve_lower(factor, values):
    return lax.linalg.triangular_solve(factor, values, left_side=True, lower=True)


def rayleigh_ritz(gram_b, gram_a):
    factor_b = jnp.linalg.cholesky(gram_b)
    symmetric = 0.5 * (gram_a + gram_a.T)
    halfway = solve_lower(factor_b, symmetric)
    return solve_lower(factor_b, halfway.T)


def operate(vectors, padded, adjacency_tiles, column_position, placing, span_tiles):
    channels, rows_here = vectors.shape
    tile_size = adjacency_tiles.shape[1]
    column_blocks = padded.reshape(channels, span_tiles, tile_size)
    gathered = jnp.take(column_blocks, column_position, axis=1)
    products = jnp.einsum(
        "cta,tab->ctb", gathered, adjacency_tiles, precision=lax.Precision.HIGHEST
    )
    summed = jnp.einsum("ctb,tr->crb", products, placing, precision=lax.Precision.HIGHEST)
    return vectors - summed.reshape(channels, rows_here)


def body(current_block, previous_block, adjacency_tiles, tile_rows, tile_cols, tile_count, locked):
    vectors_k, rows_here = current_block.shape
    tile_size = adjacency_tiles.shape[1]
    row_tiles = rows_here // tile_size
    slot_count = adjacency_tiles.shape[0]
    vertex_total = rows_here * lax.axis_size(("rows", "cols", "sub"))
    position = lax.axis_index(("rows", "cols", "sub"))
    reach_tiles = row_tiles // 2
    span_tiles = row_tiles + 2 * reach_tiles
    column_position = tile_cols - (position * row_tiles - reach_tiles)
    row_slot = tile_rows - position * row_tiles
    live_mask = (jnp.arange(slot_count, dtype=jnp.int32) < tile_count[0]).astype(jnp.float32)
    placing = (row_slot[:, None] == jnp.arange(row_tiles, dtype=jnp.int32)[None, :]).astype(
        jnp.float32
    )
    placing = placing * live_mask[:, None]
    stacked = jnp.concatenate([current_block, previous_block], axis=0)
    padded_pair = extended(stacked, ((("rows", "cols", "sub"), 1),), reach_tiles * tile_size)
    pair_image = operate(
        stacked, padded_pair, adjacency_tiles, column_position, placing, span_tiles
    )
    x_image = pair_image[:vectors_k]
    p_image = pair_image[vectors_k:]
    frozen_rows = jnp.arange(vectors_k, dtype=jnp.int32) < locked[0]
    frozen_diag = jnp.diag(frozen_rows.astype(jnp.float32))
    zero_rows = jnp.zeros((vectors_k,), jnp.float32)
    pad_diag = jnp.diag(jnp.concatenate([zero_rows, frozen_rows.astype(jnp.float32), zero_rows]))
    cross_sum, square_sum = (
        one_axis_at_a_time(jnp.sum(current_block * x_image, axis=1), ("rows", "cols", "sub")),
        one_axis_at_a_time(jnp.sum(current_block * current_block, axis=1), ("rows", "cols", "sub")),
    )
    quotient = cross_sum / (square_sum + 1e-06)
    residual = jnp.where(frozen_rows[:, None], 0.0, x_image - quotient[:, None] * current_block)
    gram_w = (
        one_axis_at_a_time(inner_products(residual, residual), ("rows", "cols", "sub"))
        / vertex_total
        + frozen_diag
    )
    factor = jnp.linalg.cholesky(gram_w)
    w_basis = solve_lower(factor, residual)
    padded = extended(w_basis, ((("rows", "cols", "sub"), 1),), reach_tiles * tile_size)
    w_image = operate(w_basis, padded, adjacency_tiles, column_position, placing, span_tiles)
    search = jnp.concatenate([current_block, w_basis, previous_block], axis=0)
    search_image = jnp.concatenate([x_image, w_image, p_image], axis=0)
    plain_sum, image_sum = (
        one_axis_at_a_time(inner_products(search, search), ("rows", "cols", "sub")),
        one_axis_at_a_time(inner_products(search, search_image), ("rows", "cols", "sub")),
    )
    gram_b = plain_sum / vertex_total + pad_diag
    gram_a = image_sum / vertex_total
    ritz_matrix = rayleigh_ritz(gram_b, gram_a)
    return (w_basis, w_image, ritz_matrix)


def solution(mesh):
    in_specs = (
        P(None, ("graphs", "rows", "cols", "sub")),
        P(None, ("graphs", "rows", "cols", "sub")),
        P(("graphs", "rows", "cols", "sub"), None, None),
        P(("graphs", "rows", "cols", "sub")),
        P(("graphs", "rows", "cols", "sub")),
        P(("graphs", "rows", "cols", "sub")),
        P("graphs"),
    )
    out_specs = (
        P(None, ("graphs", "rows", "cols", "sub")),
        P(None, ("graphs", "rows", "cols", "sub")),
        P("graphs", None),
    )
    return jax.shard_map(body, mesh=mesh, in_specs=in_specs, out_specs=out_specs, check_vma=False)
```

profile of v0, /device:TPU:33, one launch (start us, length us, event | category | flops | bytes accessed | tf_op | source)
XLA Modules:
  0.0 362.2 jit_solution(13121580219357382442)
XLA Ops:
  0.6 1.1 constant_dynamic-update-slice_fusion.1
  1.7 0.9 constant_dynamic-update-slice_fusion
  2.6 0.7 fusion.54
  3.3 4.6 %collective-permute-start = (f32[32,1024]{1,0:T(8,128)}, f32[32,1024]{1,0:T(8,128)}, u32[]{:S(2)}, u32[]{:S(2)}) collective-permute-start(f32[32,1024]{1,0:T(8,128)} %get-tuple-element.22), channel_id=1, source_target_pairs={{0,1},{1,2},{2,3},{3,4},{4,5},{5,6},{6,7},{7,8},{8,9},{9,10},{10,1... | collective-permute-start | bytes 393224 | tf_op jit(solution)/shard_map/ppermute | solution.py:15
  7.9 40.7 %collective-permute-start.1 = (f32[32,1024]{1,0:T(8,128)S(1)}, f32[32,1024]{1,0:T(8,128)}, u32[]{:S(2)}, u32[]{:S(2)}) collective-permute-start(f32[32,1024]{1,0:T(8,128)S(1)} %get-tuple-element.23), channel_id=1, source_target_pairs={{1,0},{2,1},{3,2},{4,3},{5,4},{6,5},{7,6},{8,7},{9,8},{10,9},{11,1... | collective-permute-start | bytes 393224 | tf_op jit(solution)/shard_map/ppermute | solution.py:16
  48.6 0.7 broadcast_subtract_fusion
  50.6 0.5 iota_compare_fusion.7
  51.1 0.7 compare_and_fusion
  51.8 0.6 pad_maximum_fusion.3
  52.5 1.8 copy_bitcast_fusion
  54.3 2.5 gather_fusion
  56.8 4.0 %fusion.2 = f32[48,32,128]{2,1,0:T(8,128)S(1)} fusion(f32[48,128,128]{2,1,0:T(8,128)S(1)} %copy-done, f32[48,32,128]{2,1,0:T(8,128)} %gather_fusion, pred[48]{0:T(512)(128)(4,1)S(1)} %get-tuple-element.18), kind=kOutput, calls=%fused_computation.5 | convolution fusion | flops 302186496 | bytes 4718640 | tf_op jit(solution)/shard_map/cta,tab->ctb/dot_general | solution.py:53
  60.8 0.9 fusion
  61.8 0.7 copy-done.1
  62.5 0.8 multiply_reduce_fusion
  63.3 43.8 %all-reduce.1 = (f32[16]{0:T(128)S(1)}, f32[16]{0:T(128)S(1)}) all-reduce(f32[16]{0:T(128)S(1)} %get-tuple-element.5, f32[16]{0:T(128)S(1)} %get-tuple-element.4), channel_id=1, replica_groups=mesh['graphs'=2,'rows'=32,'cols'=4,'sub'=2] {'rows'}, use_global_device_ids=true, to_apply=%region_1.2 | all-reduce | flops 32 | bytes 256 | tf_op jit(solution)/shard_map/psum | solution.py:29
  107.1 8.0 %all-reduce.3 = (f32[16]{0:T(128)S(1)}, f32[16]{0:T(128)S(1)}) all-reduce(f32[16]{0:T(128)S(1)} %get-tuple-element.8, f32[16]{0:T(128)S(1)} %get-tuple-element.9), channel_id=1, replica_groups=mesh['graphs'=2,'rows'=32,'cols'=4,'sub'=2] {'cols'}, use_global_device_ids=true, to_apply=%region_2.3 | all-reduce | flops 32 | bytes 256 | tf_op jit(solution)/shard_map/psum | solution.py:29
  115.2 19.1 %all-reduce.5 = (f32[16]{0:T(128)S(1)}, f32[16]{0:T(128)S(1)}) all-reduce(f32[16]{0:T(128)S(1)} %get-tuple-element.12, f32[16]{0:T(128)S(1)} %get-tuple-element.13), channel_id=1, replica_groups=mesh['graphs'=2,'rows'=32,'cols'=4,'sub'=2] {'sub'}, use_global_device_ids=true, to_apply=%region_3.4 | all-reduce | flops 32 | bytes 256 | tf_op jit(solution)/shard_map/psum | solution.py:29
  134.3 1.3 fusion.53
  135.6 40.0 %psum.111 = f32[16,16]{1,0:T(8,128)S(1)} all-reduce(f32[16,16]{1,0:T(8,128)S(1)} %fusion.53), channel_id=1, replica_groups=mesh['graphs'=2,'rows'=32,'cols'=4,'sub'=2] {'rows'}, use_global_device_ids=true, to_apply=%region_8.9 | all-reduce | flops 256 | bytes 2048 | tf_op jit(solution)/shard_map/psum | solution.py:29
  175.7 6.9 %psum.112 = f32[16,16]{1,0:T(8,128)S(1)} all-reduce(f32[16,16]{1,0:T(8,128)S(1)} %psum.111), channel_id=1, replica_groups=mesh['graphs'=2,'rows'=32,'cols'=4,'sub'=2] {'cols'}, use_global_device_ids=true, to_apply=%region_9.10 | all-reduce | flops 256 | bytes 2048 | tf_op jit(solution)/shard_map/psum | solution.py:29
  182.6 18.4 %psum.113 = f32[16,16]{1,0:T(8,128)S(1)} all-reduce(f32[16,16]{1,0:T(8,128)S(1)} %psum.112), channel_id=1, replica_groups=mesh['graphs'=2,'rows'=32,'cols'=4,'sub'=2] {'sub'}, use_global_device_ids=true, to_apply=%region_10.11 | all-reduce | flops 256 | bytes 2048 | tf_op jit(solution)/shard_map/psum | solution.py:29
  201.0 0.7 select_add_fusion.1
  201.8 0.7 fusion.34
  202.5 1.4 cholesky.31
  204.0 0.6 compare_reduce_fusion.1
  204.7 0.7 fusion.31
  205.3 1.2 custom-call.12
  206.5 1.3 fusion.32
  207.9 2.9 collective-permute-start.2
  210.8 2.0 collective-permute-start.3
  212.8 2.0 fusion.20
  214.8 1.6 collective-permute-done.3
  216.4 0.7 copy_bitcast_fusion.1
  217.1 2.3 gather_fusion.1
  219.4 3.8 %fusion.14 = f32[48,16,128]{2,1,0:T(8,128)S(1)} fusion(f32[48,128,128]{2,1,0:T(8,128)S(1)} %copy-done, f32[48,16,128]{2,1,0:T(8,128)} %gather_fusion.1, pred[48]{0:T(512)(128)(4,1)S(1)} %get-tuple-element.18), kind=kOutput, calls=%fused_computation.20 | convolution fusion | flops 151093248 | bytes 3932208 | tf_op jit(solution)/shard_map/cta,tab->ctb/dot_general | solution.py:53
  223.3 0.4 fusion.12
  223.8 0.6 copy-done.5
  224.4 1.1 fusion.6
  225.5 78.5 %all-reduce = (f32[48,48]{0,1:T(8,128)S(1)}, f32[48,48]{0,1:T(8,128)S(1)}) all-reduce(f32[48,48]{0,1:T(8,128)} %fusion.6, f32[48,48]{0,1:T(8,128)} %fusion.20), channel_id=1, replica_groups=mesh['graphs'=2,'rows'=32,'cols'=4,'sub'=2] {'rows'}, use_global_device_ids=true, to_apply=%region_18.19 | all-reduce | flops 4608 | bytes 36864 | tf_op jit(solution)/shard_map/psum | solution.py:29
  304.0 14.9 %all-reduce.2 = (f32[48,48]{0,1:T(8,128)S(1)}, f32[48,48]{0,1:T(8,128)S(1)}) all-reduce(f32[48,48]{0,1:T(8,128)S(1)} %get-tuple-element.6, f32[48,48]{0,1:T(8,128)S(1)} %get-tuple-element.7), channel_id=1, replica_groups=mesh['graphs'=2,'rows'=32,'cols'=4,'sub'=2] {'cols'}, use_global_device_ids=true, to_apply=%region_19.20 | all-reduce | flops 4608 | bytes 36864 | tf_op jit(solution)/shard_map/psum | solution.py:29
  318.8 32.5 %all-reduce.4 = (f32[48,48]{0,1:T(8,128)S(1)}, f32[48,48]{0,1:T(8,128)S(1)}) all-reduce(f32[48,48]{0,1:T(8,128)S(1)} %get-tuple-element.10, f32[48,48]{0,1:T(8,128)S(1)} %get-tuple-element.11), channel_id=1, replica_groups=mesh['graphs'=2,'rows'=32,'cols'=4,'sub'=2] {'sub'}, use_global_device_ids=true, to_apply=%region_20.21 | all-reduce | flops 4608 | bytes 36864 | tf_op jit(solution)/shard_map/psum | solution.py:29
  351.7 4.4 %cholesky.65 = f32[48,48]{1,0:T(8,128)S(1)} custom-call(f32[48,48]{1,0:T(8,128)S(1)} %fusion.29), custom_call_target="Cholesky" | custom-call | tf_op jit(solution)/shard_map/jit(cholesky)/cholesky | solution.py:42
  356.1 0.6 compare_reduce_fusion
  356.7 0.7 fusion.23
  357.4 3.7 %custom-call.15 = f32[1,48,48]{1,2,0:T(8,128)S(1)} custom-call(f32[1,48,48]{2,1,0:T(8,128)S(1)} %fusion.23), custom_call_target="InvertDiagBlocksLowerTriangular" | custom-call | tf_op jit(solution)/shard_map/triangular_solve/custom-call.3 | solution.py:38
  361.1 0.2 convolution_bitcast_fusion
  361.4 0.8 fusion.27
  (46 shorter events, 0.8 us)
Async XLA Ops:
  0.6 56.2 %copy-start = (f32[48,128,128]{2,1,0:T(8,128)S(1)}, f32[48,128,128]{2,1,0:T(8,128)}, u32[]{:S(2)}) copy-start(f32[48,128,128]{2,1,0:T(8,128)} %param.11) | copy-start | bytes 9437188
  3.3 49.1 %collective-permute-start = (f32[32,1024]{1,0:T(8,128)}, f32[32,1024]{1,0:T(8,128)}, u32[]{:S(2)}, u32[]{:S(2)}) collective-permute-start(f32[32,1024]{1,0:T(8,128)} %get-tuple-element.22), channel_id=1, source_target_pairs={{0,1},{1,2},{2,3},{3,4},{4,5},{5,6},{6,7},{7,8},{8,9},{9,10},{10,1... | collective-permute-start | bytes 393224 | tf_op jit(solution)/shard_map/ppermute | solution.py:15
  7.9 44.6 %collective-permute-start.1 = (f32[32,1024]{1,0:T(8,128)S(1)}, f32[32,1024]{1,0:T(8,128)}, u32[]{:S(2)}, u32[]{:S(2)}) collective-permute-start(f32[32,1024]{1,0:T(8,128)S(1)} %get-tuple-element.23), channel_id=1, source_target_pairs={{1,0},{2,1},{3,2},{4,3},{5,4},{6,5},{7,6},{8,7},{9,8},{10,9},{11,1... | collective-permute-start | bytes 393224 | tf_op jit(solution)/shard_map/ppermute | solution.py:16
  49.3 11.5 %copy-start.7 = (s32[48]{0:T(128)}, s32[48]{0:T(128)S(1)}, u32[]{:S(2)}) copy-start(s32[48]{0:T(128)S(1)} %broadcast_subtract_fusion) | copy-start | bytes 580
  50.0 10.8 %copy-start.9 = (f32[48]{0:T(128)}, f32[48]{0:T(128)S(1)}, u32[]{:S(2)}) copy-start(f32[48]{0:T(128)S(1)} %compare_convert_fusion) | copy-start | bytes 580
  51.1 1.3 copy-start.13
  56.8 5.7 %copy-start.2 = (f32[16,2048]{1,0:T(8,128)S(1)}, f32[16,2048]{1,0:T(8,128)}, u32[]{:S(2)}) copy-start(f32[16,2048]{1,0:T(8,128)} %param.9) | copy-start | bytes 393220
  61.8 0.7 copy-start.1
  134.3 70.4 %copy-start.12 = (f32[16]{0:T(128)}, f32[16]{0:T(128)S(1)}, u32[]{:S(2)}) copy-start(f32[16]{0:T(128)S(1)} %add_divide_fusion) | copy-start | bytes 196
  207.8 15.9 %copy-start.3 = (f32[16,2048]{1,0:T(8,128)}, f32[16,2048]{1,0:T(8,128)S(1)}, u32[]{:S(2)}) copy-start(f32[16,2048]{1,0:T(8,128)S(1)} %fusion.32) | copy-start | bytes 393220
  207.8 15.4 %copy-start.8 = (s32[48]{0:T(128)S(1)}, s32[48]{0:T(128)}, u32[]{:S(2)}) copy-start(s32[48]{0:T(128)} %copy-done.7) | copy-start | bytes 580
  207.8 15.4 %copy-start.10 = (f32[48]{0:T(128)S(1)}, f32[48]{0:T(128)}, u32[]{:S(2)}) copy-start(f32[48]{0:T(128)} %copy-done.9) | copy-start | bytes 580
  207.9 6.9 %collective-permute-start.2 = (f32[16,1024]{1,0:T(8,128)S(1)}, f32[16,1024]{1,0:T(8,128)S(1)}, u32[]{:S(2)}, u32[]{:S(2)}) collective-permute-start(f32[16,1024]{1,0:T(8,128)S(1)} %get-tuple-element.24), channel_id=1, source_target_pairs={{0,1},{1,2},{2,3},{3,4},{4,5},{5,6},{6,7},{7,8},{8,9},{9,10},{10,1... | collective-permute-start | bytes 196616 | tf_op jit(solution)/shard_map/ppermute | solution.py:15
  210.8 5.6 %collective-permute-start.3 = (f32[16,1024]{1,0:T(8,128)S(1)}, f32[16,1024]{1,0:T(8,128)S(1)}, u32[]{:S(2)}, u32[]{:S(2)}) collective-permute-start(f32[16,1024]{1,0:T(8,128)S(1)} %get-tuple-element.25), channel_id=1, source_target_pairs={{1,0},{2,1},{3,2},{4,3},{5,4},{6,5},{7,6},{8,7},{9,8},{10,9},{11,1... | collective-permute-start | bytes 196616 | tf_op jit(solution)/shard_map/ppermute | solution.py:16
  219.4 5.0 %copy-start.4 = (f32[16,2048]{1,0:T(8,128)S(1)}, f32[16,2048]{1,0:T(8,128)}, u32[]{:S(2)}) copy-start(f32[16,2048]{1,0:T(8,128)} %get-tuple-element.21) | copy-start | bytes 393220
  219.4 5.0 %copy-start.6 = (f32[16,2048]{1,0:T(8,128)S(1)}, f32[16,2048]{1,0:T(8,128)}, u32[]{:S(2)}) copy-start(f32[16,2048]{1,0:T(8,128)} %param.10) | copy-start | bytes 393220
  219.4 132.0 %copy-start.11 = (f32[48]{0:T(128)S(1)}, f32[48]{0:T(128)}, u32[]{:S(2)}) copy-start(f32[48]{0:T(128)} %pad_maximum_fusion.3) | copy-start | bytes 580
  223.7 0.7 copy-start.5
where the time goes:
time: 363 us; the launch traced here: 362 us
  blocking collectives  262 us (72%)
  starting transfers between devices  50.2 us (14%)
  other arithmetic  21 us (6%)
  matrix products  15.9 us (4%)
  local copies, waits for them, and re-layouts  9.13 us (3%)
    psum x9, blocking collectives, one_axis_at_a_time(): value = lax.psum(value, axis)  262 us
    ppermute x2, starting transfers between devices, extended(): lax.ppermute(initial, axis, [(b, a) for a, b in up])  42.7 us
    dot_general x2, matrix products, operate(): jnp.einsum('cta,tab->ctb', gathered, adjacency_tiles, precision=lax.Preci...  7.81 us
    ppermute x2, starting transfers between devices, extended(): lax.ppermute(last, axis, up)  7.51 us
  transfers between devices with their start and end apart: 4, of which 1 were waited for; matrix products, arithmetic and copies ran while one was open for 1% of the time, Pallas kernels for 0%

commit v1 on v0

--- a/solution.py
+++ b/solution.py
@@ -26,7 +26,7 @@
 
 def one_axis_at_a_time(value, axes):
     for axis in axes:
-        value = lax.psum(value, axis)
+        value = jnp.sum(lax.all_gather(value, axis), axis=0)
     return value
 
 

time: 363 us -> 404 us (1.11)
  blocking collectives: 262 us -> 292 us
  local copies, waits for them, and re-layouts: 9.13 us -> 15 us
  other arithmetic: 21 us -> 26.3 us
    psum x9 -> x0, blocking collectives: 262 us -> none  [one_axis_at_a_time(): value = lax.psum(value, axis)]
    all_gather x0 -> x9, blocking collectives: none -> 221 us  [one_axis_at_a_time(): value = jnp.sum(lax.all_gather(value, axis), axis=0)]
    unnamed x0 -> x3, blocking collectives: none -> 70.9 us
    unnamed x29 -> x44, local copies, waits for them, and re-layouts: 2.45 us -> 7.12 us
  transfers between devices with their start and end apart: 4 -> 4, of which waited for: 1 -> 0; matrix products, arithmetic and copies ran while one was open for 1% -> 3% of each run, Pallas kernels for 0% -> 0%
where the time goes in v1:
time: 404 us; the launch traced here: 403 us
  blocking collectives  292 us (72%)
  starting transfers between devices  49.9 us (12%)
  other arithmetic  26.3 us (7%)
  matrix products  16.2 us (4%)
  local copies, waits for them, and re-layouts  15 us (4%)
  between operations  4.1 us (1%)
    all_gather x9, blocking collectives, one_axis_at_a_time(): value = jnp.sum(lax.all_gather(value, axis), axis=0)  221 us
    unnamed x3, blocking collectives  70.9 us
    ppermute x2, starting transfers between devices, extended(): lax.ppermute(initial, axis, [(b, a) for a, b in up])  43.3 us
  transfers between devices with their start and end apart: 4, of which 0 were waited for; matrix products, arithmetic and copies ran while one was open for 3% of the time, Pallas kernels for 0%

profile of v1, /device:TPU:33, one launch (start us, length us, event | category | flops | bytes accessed | tf_op | source)
XLA Modules:
  0.0 403.1 jit_solution(12607340085229440633)
XLA Ops:
  0.6 1.1 constant_dynamic-update-slice_fusion.1
  1.7 0.9 constant_dynamic-update-slice_fusion
  2.6 0.7 fusion.52
  3.3 4.6 %collective-permute-start = (f32[32,1024]{1,0:T(8,128)}, f32[32,1024]{1,0:T(8,128)}, u32[]{:S(2)}, u32[]{:S(2)}) collective-permute-start(f32[32,1024]{1,0:T(8,128)} %get-tuple-element.16), channel_id=1, source_target_pairs={{0,1},{1,2},{2,3},{3,4},{4,5},{5,6},{6,7},{7,8},{8,9},{9,10},{10,1... | collective-permute-start | bytes 393224 | tf_op jit(solution)/shard_map/ppermute | solution.py:15
  7.9 40.7 %collective-permute-start.1 = (f32[32,1024]{1,0:T(8,128)S(1)}, f32[32,1024]{1,0:T(8,128)}, u32[]{:S(2)}, u32[]{:S(2)}) collective-permute-start(f32[32,1024]{1,0:T(8,128)S(1)} %get-tuple-element.17), channel_id=1, source_target_pairs={{1,0},{2,1},{3,2},{4,3},{5,4},{6,5},{7,6},{8,7},{9,8},{10,9},{11,1... | collective-permute-start | bytes 393224 | tf_op jit(solution)/shard_map/ppermute | solution.py:16
  48.6 0.7 broadcast_subtract_fusion
  51.2 1.2 compare_and_fusion
  53.0 1.3 dynamic-slice
  54.2 1.3 dynamic-slice.1
  56.9 1.2 dynamic-slice.2
  58.7 0.7 pad_clamp_fusion
  59.3 1.8 copy_bitcast_fusion
  61.2 2.5 gather_fusion
  63.7 4.0 convolution_bitcast_fusion
  67.7 0.9 fusion.1
  68.7 0.7 copy-done.1
  69.4 0.9 multiply_reduce_fusion
  70.7 43.3 %all-reduce.6 = (f32[512]{0:T(512)S(1)}, f32[512]{0:T(512)S(1)}) all-reduce(f32[512]{0:T(512)S(1)} %dynamic-update-slice.6, f32[512]{0:T(512)S(1)} %dynamic-update-slice.9), channel_id=2, replica_groups=mesh['graphs'=2,'rows'=32,'cols'=4,'sub'=2] {'rows'}, use_global_device_ids=true, to_apply=%add | all-reduce | flops 1024 | bytes 8192
  114.7 8.1 %all-reduce.7 = (f32[64]{0:T(128)S(1)}, f32[64]{0:T(128)S(1)}) all-reduce(f32[64]{0:T(128)S(1)} %dynamic-update-slice.7, f32[64]{0:T(128)S(1)} %dynamic-update-slice.10), channel_id=3, replica_groups=mesh['graphs'=2,'rows'=32,'cols'=4,'sub'=2] {'cols'}, use_global_device_ids=true, to_apply=%add.1 | all-reduce | flops 128 | bytes 1024
  123.5 19.5 %all-reduce.8 = (f32[32]{0:T(128)S(1)}, f32[32]{0:T(128)S(1)}) all-reduce(f32[32]{0:T(128)S(1)} %dynamic-update-slice.8, f32[32]{0:T(128)S(1)} %dynamic-update-slice.11), channel_id=4, replica_groups=mesh['graphs'=2,'rows'=32,'cols'=4,'sub'=2] {'sub'}, use_global_device_ids=true, to_apply=%add.2 | all-reduce | flops 64 | bytes 512
  143.2 1.3 fusion.51
  144.5 38.8 %all-gather.6 = f32[512,16]{1,0:T(8,128)S(1)} all-gather(f32[16,16]{1,0:T(8,128)S(1)} %fusion.51), channel_id=8, replica_groups=mesh['graphs'=2,'rows'=32,'cols'=4,'sub'=2] {'rows'}, dimensions={0}, use_global_device_ids=true | all-gather | bytes 33792 | tf_op jit(solution)/shard_map/all_gather | solution.py:29
  183.3 9.1 %all-gather.7 = f32[64,16]{1,0:T(8,128)S(1)} all-gather(f32[16,16]{1,0:T(8,128)S(1)} %reduce_sum.163), channel_id=9, replica_groups=mesh['graphs'=2,'rows'=32,'cols'=4,'sub'=2] {'cols'}, dimensions={0}, use_global_device_ids=true | all-gather | bytes 5120 | tf_op jit(solution)/shard_map/all_gather | solution.py:29
  192.4 18.7 %all-gather.8 = f32[32,16]{1,0:T(8,128)S(1)} all-gather(f32[16,16]{1,0:T(8,128)S(1)} %reduce_sum.164), channel_id=10, replica_groups=mesh['graphs'=2,'rows'=32,'cols'=4,'sub'=2] {'sub'}, dimensions={0}, use_global_device_ids=true | all-gather | bytes 3072 | tf_op jit(solution)/shard_map/all_gather | solution.py:29
  211.3 0.8 fusion.32
  212.0 1.4 cholesky.31
  214.8 1.2 custom-call.12
  216.1 1.3 fusion.29
  217.3 1.5 fusion.16
  219.5 49.2 %all-gather.9 = f32[1536,48]{1,0:T(8,128)} all-gather(f32[48,48]{1,0:T(8,128)S(1)} %fusion.16), channel_id=11, replica_groups=mesh['graphs'=2,'rows'=32,'cols'=4,'sub'=2] {'rows'}, dimensions={0}, use_global_device_ids=true | all-gather | bytes 304128 | tf_op jit(solution)/shard_map/all_gather | solution.py:29
  268.6 1.2 reduce_sum.166
  269.8 9.8 %all-gather.10 = f32[192,48]{1,0:T(8,128)S(1)} all-gather(f32[48,48]{1,0:T(8,128)S(1)} %reduce_sum.166), channel_id=12, replica_groups=mesh['graphs'=2,'rows'=32,'cols'=4,'sub'=2] {'cols'}, dimensions={0}, use_global_device_ids=true | all-gather | bytes 46080 | tf_op jit(solution)/shard_map/all_gather | solution.py:29
  279.6 17.7 %all-gather.11 = f32[96,48]{1,0:T(8,128)S(1)} all-gather(f32[48,48]{1,0:T(8,128)S(1)} %reduce_sum.167), channel_id=13, replica_groups=mesh['graphs'=2,'rows'=32,'cols'=4,'sub'=2] {'sub'}, dimensions={0}, use_global_device_ids=true | all-gather | bytes 27648 | tf_op jit(solution)/shard_map/all_gather | solution.py:29
  297.5 0.8 fusion.26
  298.3 4.4 %cholesky.65 = f32[48,48]{1,0:T(8,128)S(1)} custom-call(f32[48,48]{1,0:T(8,128)S(1)} %fusion.26), custom_call_target="Cholesky" | custom-call | tf_op jit(solution)/shard_map/jit(cholesky)/cholesky | solution.py:42
  303.3 1.9 collective-permute-start.2
  305.3 2.6 collective-permute-start.3
  307.9 0.7 fusion.19
  308.6 4.3 %custom-call.15 = f32[1,48,48]{1,2,0:T(8,128)} custom-call(f32[1,48,48]{2,1,0:T(8,128)S(1)} %fusion.19), custom_call_target="InvertDiagBlocksLowerTriangular" | custom-call | tf_op jit(solution)/shard_map/triangular_solve/custom-call.3 | solution.py:38
  312.9 1.6 copy_bitcast_fusion.1
  314.4 2.3 gather_fusion.1
  316.7 3.8 convolution_bitcast_fusion.1
  321.7 47.8 %all-gather.12 = f32[1536,48]{1,0:T(8,128)} all-gather(f32[48,48]{1,0:T(8,128)S(1)} %fusion.4), channel_id=14, replica_groups=mesh['graphs'=2,'rows'=32,'cols'=4,'sub'=2] {'rows'}, dimensions={0}, use_global_device_ids=true | all-gather | bytes 304128 | tf_op jit(solution)/shard_map/all_gather | solution.py:29
  369.5 1.2 reduce_sum.169
  370.7 10.8 %all-gather.13 = f32[192,48]{1,0:T(8,128)S(1)} all-gather(f32[48,48]{1,0:T(8,128)S(1)} %reduce_sum.169), channel_id=15, replica_groups=mesh['graphs'=2,'rows'=32,'cols'=4,'sub'=2] {'cols'}, dimensions={0}, use_global_device_ids=true | all-gather | bytes 46080 | tf_op jit(solution)/shard_map/all_gather | solution.py:29
  381.5 19.0 %all-gather.14 = f32[96,48]{1,0:T(8,128)S(1)} all-gather(f32[48,48]{1,0:T(8,128)S(1)} %reduce_sum.170), channel_id=16, replica_groups=mesh['graphs'=2,'rows'=32,'cols'=4,'sub'=2] {'sub'}, dimensions={0}, use_global_device_ids=true | all-gather | bytes 27648 | tf_op jit(solution)/shard_map/all_gather | solution.py:29
  400.6 1.0 convolution_bitcast_fusion.2
  401.6 1.6 fusion.23
  (85 shorter events, 7.5 us)
Async XLA Ops:
  0.6 63.1 %copy-start = (f32[48,128,128]{2,1,0:T(8,128)S(1)}, f32[48,128,128]{2,1,0:T(8,128)}, u32[]{:S(2)}) copy-start(f32[48,128,128]{2,1,0:T(8,128)} %param.11) | copy-start | bytes 9437188
  3.3 56.0 %collective-permute-start = (f32[32,1024]{1,0:T(8,128)}, f32[32,1024]{1,0:T(8,128)}, u32[]{:S(2)}, u32[]{:S(2)}) collective-permute-start(f32[32,1024]{1,0:T(8,128)} %get-tuple-element.16), channel_id=1, source_target_pairs={{0,1},{1,2},{2,3},{3,4},{4,5},{5,6},{6,7},{7,8},{8,9},{9,10},{10,1... | collective-permute-start | bytes 393224 | tf_op jit(solution)/shard_map/ppermute | solution.py:15
  7.9 51.4 %collective-permute-start.1 = (f32[32,1024]{1,0:T(8,128)S(1)}, f32[32,1024]{1,0:T(8,128)}, u32[]{:S(2)}, u32[]{:S(2)}) collective-permute-start(f32[32,1024]{1,0:T(8,128)S(1)} %get-tuple-element.17), channel_id=1, source_target_pairs={{1,0},{2,1},{3,2},{4,3},{5,4},{6,5},{7,6},{8,7},{9,8},{10,9},{11,1... | collective-permute-start | bytes 393224 | tf_op jit(solution)/shard_map/ppermute | solution.py:16
  49.3 18.4 %copy-start.8 = (s32[48]{0:T(128)}, s32[48]{0:T(128)S(1)}, u32[]{:S(2)}) copy-start(s32[48]{0:T(128)S(1)} %broadcast_subtract_fusion) | copy-start | bytes 580
  50.0 17.7 %copy-start.10 = (f32[48]{0:T(128)}, f32[48]{0:T(128)S(1)}, u32[]{:S(2)}) copy-start(f32[48]{0:T(128)S(1)} %compare_convert_fusion) | copy-start | bytes 580
  51.2 7.5 %copy-start.13 = (f32[16]{0:T(128)}, f32[16]{0:T(128)S(1)}, u32[]{:S(2)}) copy-start(f32[16]{0:T(128)S(1)} %fusion.50) | copy-start | bytes 196
  63.7 5.7 %copy-start.2 = (f32[16,2048]{1,0:T(8,128)S(1)}, f32[16,2048]{1,0:T(8,128)}, u32[]{:S(2)}) copy-start(f32[16,2048]{1,0:T(8,128)} %param.9) | copy-start | bytes 393220
  68.7 0.7 copy-start.1
  143.2 40.1 %copy-start.12 = (f32[16]{0:T(128)}, f32[16]{0:T(128)S(1)}, u32[]{:S(2)}) copy-start(f32[16]{0:T(128)S(1)} %add_divide_fusion) | copy-start | bytes 196
  217.3 103.7 %copy-start.3 = (f32[16,2048]{1,0:T(8,128)}, f32[16,2048]{1,0:T(8,128)S(1)}, u32[]{:S(2)}) copy-start(f32[16,2048]{1,0:T(8,128)S(1)} %fusion.29) | copy-start | bytes 393220
  269.8 50.7 %copy-start.9 = (s32[48]{0:T(128)S(1)}, s32[48]{0:T(128)}, u32[]{:S(2)}) copy-start(s32[48]{0:T(128)} %copy-done.8) | copy-start | bytes 580
  269.8 50.7 %copy-start.11 = (f32[48]{0:T(128)S(1)}, f32[48]{0:T(128)}, u32[]{:S(2)}) copy-start(f32[48]{0:T(128)} %copy-done.10) | copy-start | bytes 580
  303.3 9.5 %collective-permute-start.2 = (f32[16,1024]{1,0:T(8,128)}, f32[16,1024]{1,0:T(8,128)S(1)}, u32[]{:S(2)}, u32[]{:S(2)}) collective-permute-start(f32[16,1024]{1,0:T(8,128)} %get-tuple-element.18), channel_id=1, source_target_pairs={{0,1},{1,2},{2,3},{3,4},{4,5},{5,6},{6,7},{7,8},{8,9},{9,10},{10,1... | collective-permute-start | bytes 196616 | tf_op jit(solution)/shard_map/ppermute | solution.py:15
  305.3 7.6 %collective-permute-start.3 = (f32[16,1024]{1,0:T(8,128)}, f32[16,1024]{1,0:T(8,128)}, u32[]{:S(2)}, u32[]{:S(2)}) collective-permute-start(f32[16,1024]{1,0:T(8,128)} %get-tuple-element.19), channel_id=1, source_target_pairs={{1,0},{2,1},{3,2},{4,3},{5,4},{6,5},{7,6},{8,7},{9,8},{10,9},{11,1... | collective-permute-start | bytes 196616 | tf_op jit(solution)/shard_map/ppermute | solution.py:16
  316.7 4.4 %copy-start.4 = (f32[16,2048]{1,0:T(8,128)S(1)}, f32[16,2048]{1,0:T(8,128)}, u32[]{:S(2)}) copy-start(f32[16,2048]{1,0:T(8,128)} %get-tuple-element.14) | copy-start | bytes 393220
  316.7 4.4 %copy-start.5 = (f32[16,2048]{1,0:T(8,128)S(1)}, f32[16,2048]{1,0:T(8,128)}, u32[]{:S(2)}) copy-start(f32[16,2048]{1,0:T(8,128)} %get-tuple-element.15) | copy-start | bytes 393220
  316.7 4.4 %copy-start.7 = (f32[16,2048]{1,0:T(8,128)S(1)}, f32[16,2048]{1,0:T(8,128)}, u32[]{:S(2)}) copy-start(f32[16,2048]{1,0:T(8,128)} %param.10) | copy-start | bytes 393220
  321.1 0.7 copy-start.6
